TPU v7x, 32 devices: a whole 2x2x4 slice. The times are simulated.
32 devices in a mesh: south: 2 (over core), east: 4 (over z), down: 2 (over x), ens: 2 (over y).
Axes of the slice: x: 2, y: 2, z: 4, core: 2. Of those that a mesh axis runs over, the one named last changes fastest.
Arguments:
- density: float32 [16, 128, 128, 128], P(('ens', 'south'), 'east', 'down'), parts along dimension 0, may hold values from 0.2 to 1.8
- flow_j: float32 [16, 128, 128, 128], P(('ens', 'south'), 'east', 'down'), parts along dimension 0, may hold values from -0.3 to 0.3
- flow_i: float32 [16, 128, 128, 128], P(('ens', 'south'), 'east', 'down'), parts along dimension 0, may hold values from -0.3 to 0.3
- flow_k: float32 [16, 128, 128, 128], P(('ens', 'south'), 'east', 'down'), parts along dimension 0, may hold values from -0.3 to 0.3
Outputs:
- density_end: float32 [16, 128, 128, 128], P(('ens', 'south'), 'east', 'down'), parts along dimension 0
There are 2 independent parts, one for each index of `ens`. A program takes and returns all parts, laid end to end along the dimension named above; each array names one. Nothing has to cross between parts.
All inputs are finite; a program needn't handle non-finite values.
Results may differ from a plain program's by a relative error of at most 0.00002.
Values sent between devices are 32-bit elements; how exact they have to be, the bound alone decides.
A program may use at most 192 MiB of HBM per device.

v0:
```python
import functools

import jax
import jax.numpy as jnp
from jax import lax
from jax.experimental import pallas as pl
from jax.experimental.pallas import tpu as pltpu
from jax.sharding import PartitionSpec as P

STEPS = 3
TILE = 8
MESH = pl.DeviceIdType.MESH


def divisor(total, most):
    return max(d for d in range(1, most + 1) if total % d == 0)


def groups(low, high, size):
    return [min(at, high - size) for at in range(low, high, size)]


def kernel(
    counts, density, flow_j, flow_i, flow_k, out,
    field, cj, ci, ck, pack, land,
    load_sem, flow_sem, isend, irecv, ksend, krecv, jsend, jrecv,
):
    nj, ni, nk, lanes = density.shape
    deep = nk + 2 * TILE
    n_south, n_east, n_down = counts
    south, east, down = (lax.axis_index(a) for a in ("south", "east", "down"))
    index = {"south": south, "east": east, "down": down}
    has = {
        ("south", 0): (n_south > 1, south > 0),
        ("south", 1): (n_south > 1, south < n_south - 1),
        ("east", 0): (n_east > 1, east > 0),
        ("east", 1): (n_east > 1, east < n_east - 1),
        ("down", 0): (n_down > 1, down > 0),
        ("down", 1): (n_down > 1, down < n_down - 1),
    }
    inside_k = pl.ds(TILE, nk)
    wide = divisor(ni - 2, 6)
    blocks = (ni - 2) // wide
    cut = 1 + wide * (blocks // 2)
    pieces = [(0, cut), (cut, ni)]

    def neighbour(axis, side):
        return {axis: index[axis] + (1 if side else -1)}

    def when_has(axis, side, act):
        static, dynamic = has[axis, side]
        if static:
            pl.when(dynamic)(act)

    def when_edge(axis, side, act):
        static, dynamic = has[axis, side]
        if static:
            pl.when(jnp.logical_not(dynamic))(act)
        else:
            act()

    first = jnp.where(south == 0, 1, 0) if n_south > 1 else 0

    def plane(t):
        return first * (nj - 1 - t) + (1 - first) * t

    def load(t):
        j, inner = plane(t), pl.ds(1, ni - 2)
        return pltpu.make_async_copy(
            density.at[j, inner], field.at[0, j + 1, pl.ds(2, ni - 2), inside_k], load_sem.at[t]
        )

    def load_face(side):
        i = (ni - 1) * side
        return pltpu.make_async_copy(
            density.at[:, i], field.at[0, pl.ds(1, nj), i + 1, inside_k], load_sem.at[nj + side]
        )

    flows = ((flow_j, cj), (flow_i, ci), (flow_k, ck))

    def load_flow(t, d):
        source, target = flows[d]
        inner = pl.ds(1, ni - 2)
        return pltpu.make_async_copy(
            source.at[plane(t), inner], target.at[plane(t), inner], flow_sem.at[d, t]
        )

    def load_flow_face(side, d):
        source, target = flows[d]
        i = (ni - 1) * side
        return pltpu.make_async_copy(source.at[:, i], target.at[:, i], flow_sem.at[d, nj + side])

    def copy_i(s, side, j):
        return pltpu.make_async_remote_copy(
            src_ref=field.at[s, j + 1, ni if side else 1, inside_k],
            dst_ref=field.at[s, j + 1, 0 if side else ni + 1, inside_k],
            send_sem=isend.at[s, side, j],
            recv_sem=irecv.at[s, 1 - side, j],
            device_id=neighbour("east", side),
            device_id_type=MESH,
        )

    def copy_k(s, side, j):
        return pltpu.make_async_remote_copy(
            src_ref=pack.at[s, side, j],
            dst_ref=land.at[s, 1 - side, j],
            send_sem=ksend.at[s, side, j],
            recv_sem=krecv.at[s, 1 - side, j],
            device_id=neighbour("down", side),
            device_id_type=MESH,
        )

    def copy_j(s, side, piece):
        low, high = pieces[piece]
        rows = pl.ds(low + 1, high - low)
        return pltpu.make_async_remote_copy(
            src_ref=field.at[s, nj if side else 1, rows, inside_k],
            dst_ref=field.at[s, 0 if side else nj + 1, rows, inside_k],
            send_sem=jsend.at[s, side, piece],
            recv_sem=jrecv.at[s, 1 - side, piece],
            device_id=neighbour("south", side),
            device_id_type=MESH,
        )

    def send_i(s, t):
        for side in range(2):
            when_has("east", side, lambda side=side: copy_i(s, side, plane(t)).start())

    def send_k(s, t):
        for side in range(2):
            when_has("down", side, lambda side=side: copy_k(s, side, plane(t)).start())

    def start_j(s, side):
        for piece in range(len(pieces)):
            copy_j(s, side, piece).start()

    def send_j(s, t):
        if n_south > 1 and t == 0:
            pl.when(south == 0)(lambda: start_j(s, 1))
            pl.when(south > 0)(lambda: start_j(s, 0))
        if n_south > 2 and t == nj - 1:
            pl.when((south > 0) & (south < n_south - 1))(lambda: start_j(s, 1))

    waited = set()

    def wait_j(s, t, piece):
        if (s, t, piece) in waited:
            return
        waited.add((s, t, piece))
        if n_south > 1 and t == 0:
            pl.when(south == 0)(lambda: copy_j(s, 0, piece).wait_recv())
            pl.when(south > 0)(lambda: copy_j(s, 1, piece).wait_recv())
        if n_south > 2 and t == nj - 1:
            pl.when((south > 0) & (south < n_south - 1))(
                lambda: copy_j(s, 0, piece).wait_recv()
            )

    def wait_i(s, t):
        for side in range(2):
            when_has("east", side, lambda side=side: copy_i(s, 1 - side, plane(t)).wait_recv())

    def rows(s, j, i, count):
        def at(dj, di, dk):
            return field[s, j + 1 + dj, i + 1 + di, pl.ds(TILE + dk, nk), :]

        line = [at(0, r - 1, 0) for r in range(count + 2)]
        for r in range(count):
            cell = (j, i + r)
            lower = [at(-1, r, 0), line[r], at(0, r, -1)]
            upper = [at(1, r, 0), line[r + 2], at(0, r, 1)]
            gain = [c[cell] for c in (cj, ci, ck)]
            if s == 0:
                gain = [0.05 - g for g in gain]
                for c, g in zip((cj, ci, ck), gain):
                    c[cell] = g
            drift = [g * (u - l) for g, u, l in zip(gain, upper, lower)]
            value = (0.7 * line[r + 1] + 0.1 * (lower[0] + lower[1] + lower[2])) + (
                drift[0] + drift[1] + drift[2]
            )
            if s + 1 < STEPS:
                field[s + 1, j + 1, i + 1 + r, inside_k, :] = value
            else:
                out[cell] = value

    flat = field.reshape(STEPS, nj + 2, (ni + 2) * deep, lanes)
    flat_gain = ck.reshape(nj, ni * nk, lanes)
    flat_out = out.reshape(nj, ni * nk, lanes)

    def edge_field(s, j, i, size, side):
        row = (i + 1) * deep + TILE + (nk - 1) * side
        return flat.at[s, j + 1, pl.ds(row, size, stride=deep), :]

    def edge(ref, j, i, size, side):
        return ref.at[j, pl.ds(i * nk + (nk - 1) * side, size, stride=nk), :]

    def inner(s, t):
        j = plane(t)
        if s == 0:
            for d in range(3):
                load_flow(t, d).wait()
        edges = (t == 0) or (t == nj - 1 and n_south > 2)
        spans = [(0, blocks // 2), (blocks // 2, blocks)] if edges else [(0, blocks)]
        for piece, (low, high) in enumerate(spans):
            if edges:
                wait_j(s, t, piece)

            @pl.loop(low, high)
            def _(b):
                rows(s, j, 1 + b * wide, wide)

    def face(s, t):
        j = plane(t)
        for piece in range(len(pieces)):
            wait_j(s, t, piece)
        for side in range(2):
            def corner(side=side):
                copy_k(s, 1 - side, j).wait_recv()
                row = TILE + nk if side else TILE - 1
                for i in (0, ni - 1):
                    field[s, j + 1, i + 1, pl.ds(row, 1), :] = land[s, side, j, pl.ds(i, 1), :]
            when_has("down", side, corner)
        wait_i(s, t)
        for i in (0, ni - 1):
            rows(s, j, i, 1)
        if s + 1 < STEPS:
            send_i(s + 1, t)

    def fix(s, t):
        j = plane(t)
        for side in range(2):
            def act(side=side):
                parts = []
                for i in groups(1, ni - 1, TILE):
                    gain = edge(flat_gain, j, i, TILE, side)[...]
                    gain = gain if side else 0.1 - gain
                    if s + 1 < STEPS:
                        target = edge_field(s + 1, j, i, TILE, side)
                    else:
                        target = edge(flat_out, j, i, TILE, side)
                    value = target[...] + gain * land[s, side, j, pl.ds(i, TILE), :]
                    parts.append((i, target, value))
                for i, target, value in parts:
                    target[...] = value
                    if s + 1 < STEPS:
                        pack[s + 1, side, j, pl.ds(i, TILE), :] = value
                if s + 1 < STEPS:
                    k = TILE + (nk - 1) * side
                    for i in (0, ni - 1):
                        pack[s + 1, side, j, pl.ds(i, 1), :] = field[
                            s + 1, j + 1, i + 1, pl.ds(k, 1), :
                        ]
            when_has("down", side, act)
        if s + 1 < STEPS:
            send_k(s + 1, t)
            send_j(s + 1, t)

    barrier = pltpu.get_barrier_semaphore()
    for axis, side in has:
        def greet(axis=axis, side=side):
            pl.semaphore_signal(
                barrier, inc=1, device_id=neighbour(axis, side), device_id_type=MESH
            )
        when_has(axis, side, greet)

    for side in range(2):
        load_face(side).start()
    for t in range(nj):
        load(t).start()
    for d in range(3):
        for side in range(2):
            load_flow_face(side, d).start()
    for t in range(nj):
        for d in range(3):
            load_flow(t, d).start()

    zero_row = jnp.zeros((TILE, lanes), jnp.float32)
    zero_line = jnp.zeros((nk, lanes), jnp.float32)
    for s in range(STEPS):
        @pl.loop(0, nj)
        def _(j):
            for i in groups(0, ni, TILE):
                for row in (TILE - 1, TILE + nk):
                    flat[s, j + 1, pl.ds((i + 1) * deep + row, TILE, stride=deep), :] = zero_row

    for side in range(2):
        def zero_j(side=side):
            for s in range(STEPS):
                @pl.loop(0, ni)
                def _(i):
                    field[s, (nj + 1) * side, i + 1, inside_k, :] = zero_line

        def zero_i(side=side):
            for s in range(STEPS):
                @pl.loop(0, nj)
                def _(j):
                    field[s, j + 1, (ni + 1) * side, inside_k, :] = zero_line

        when_edge("south", side, zero_j)
        when_edge("east", side, zero_i)

    pl.semaphore_wait(barrier, sum(jnp.where(d, 1, 0) for s, d in has.values() if s))
    for side in range(2):
        load_face(side).wait()
    for t in range(nj):
        send_i(0, t)
    for t in range(nj):
        load(t).wait()
        for side in range(2):
            def first_pack(side=side):
                for i in groups(0, ni, TILE):
                    pack[0, side, plane(t), pl.ds(i, TILE), :] = edge_field(
                        0, plane(t), i, TILE, side
                    )[...]
            when_has("down", side, first_pack)
        send_k(0, t)
        send_j(0, t)
    for d in range(3):
        for side in range(2):
            load_flow_face(side, d).wait()

    inner(0, 0)
    for t in range(nj):
        if t < 2:
            face(0, t)
            fix(0, t)
            if t + 1 < min(nj, 2):
                inner(0, t + 1)
        else:
            face(0, t)
            inner(0, t)
            fix(0, t)
    inner(1, 1)
    inner(1, 0)
    for s in range(1, STEPS):
        for t in range(nj):
            face(s, t)
            fix(s, t)
            if t + 2 < nj:
                inner(s, t + 2)
            elif s + 1 < STEPS:
                if t == nj - 2 and nj > 3:
                    inner(s + 1, 1)
                if t == nj - 1:
                    if nj <= 3:
                        inner(s + 1, 1)
                    inner(s + 1, 0)

    for s in range(STEPS):
        for side in range(2):
            for piece in range(len(pieces)):
                when_has(
                    "south", side, lambda side=side, piece=piece: copy_j(s, side, piece).wait_send()
                )
            for j in range(nj):
                when_has("east", side, lambda side=side, j=j: copy_i(s, side, j).wait_send())
                when_has("down", side, lambda side=side, j=j: copy_k(s, side, j).wait_send())


def per_device(counts, density, flow_j, flow_i, flow_k):
    nj, ni, nk, lanes = density.shape
    f32 = jnp.float32
    dma = pltpu.SemaphoreType.DMA
    return pl.pallas_call(
        functools.partial(kernel, counts),
        out_shape=pltpu.VMEM(density.shape, f32),
        in_specs=[pl.BlockSpec(memory_space=pl.ANY)] * 4,
        out_specs=pl.BlockSpec(memory_space=pltpu.VMEM),
        scratch_shapes=[
            pltpu.VMEM((STEPS, nj + 2, ni + 2, nk + 2 * TILE, lanes), f32),
            pltpu.VMEM((nj, ni, nk, lanes), f32),
            pltpu.VMEM((nj, ni, nk, lanes), f32),
            pltpu.VMEM((nj, ni, nk, lanes), f32),
            pltpu.VMEM((STEPS, 2, nj, ni, lanes), f32),
            pltpu.VMEM((STEPS, 2, nj, ni, lanes), f32),
            dma((nj + 2,)),
            dma((3, nj + 2)),
            dma((STEPS, 2, nj)),
            dma((STEPS, 2, nj)),
            dma((STEPS, 2, nj)),
            dma((STEPS, 2, nj)),
            dma((STEPS, 2, 2)),
            dma((STEPS, 2, 2)),
        ],
        compiler_params=pltpu.CompilerParams(
            collective_id=0, has_side_effects=True, vmem_limit_bytes=58 * 1024 * 1024
        ),
    )(density, flow_j, flow_i, flow_k)


def solution(mesh):
    spec = P(("ens", "south"), "east", "down", None)
    counts = tuple(mesh.shape[a] for a in ("south", "east", "down"))
    return jax.shard_map(
        functools.partial(per_device, counts),
        mesh=mesh,
        in_specs=(spec,) * 4,
        out_specs=spec,
        check_vma=False,
    )
```

profile of v0, /device:TPU:0, one launch (start us, length us, event | category | flops | bytes accessed | tf_op | source)
XLA Modules:
  0.0 21.4 jit_solution(4648532352720425148)
XLA Ops:
  0.0 19.4 %shard_map.46 = f32[4,32,64,128]{3,2,1,0:T(8,128)S(1)} custom-call(f32[4,32,64,128]{3,2,1,0:T(8,128)} %density.1, f32[4,32,64,128]{3,2,1,0:T(8,128)} %flow_j.1, f32[4,32,64,128]{3,2,1,0:T(8,128)} %flow_i.1, f32[4,32,64,128]{3,2,1,0:T(8,128)} %flow_k.1), custom_call_target="tpu_custom_call" | custom-call | tf_op jit(solution)/shard_map/pallas_call | solution.py:363
  19.4 2.0 %copy.6 = f32[4,32,64,128]{3,2,1,0:T(8,128)} copy(f32[4,32,64,128]{3,2,1,0:T(8,128)S(1)} %shard_map.46) | data formatting | bytes 8388608
where the time goes:
time: 21.5 us; the launch traced here: 21.4 us
  Pallas kernels  19.4 us (90%)
  local copies, waits for them, and re-layouts  2.02 us (9%)
    pallas_call x1, Pallas kernels, per_device(): pl.pallas_call(functools.partial(kernel, counts), out_shape=pltpu.VMEM(de...  19.4 us
    unnamed x1, local copies, waits for them, and re-layouts  2.02 us

commit v1 on v0

v1 whole, which is shorter than its diff:
```python
import functools

import jax
import jax.numpy as jnp
from jax import lax
from jax.experimental import pallas as pl
from jax.experimental.pallas import tpu as pltpu
from jax.sharding import PartitionSpec as P

STEPS = 3
TILE = 8
MESH = pl.DeviceIdType.MESH
PLAN = """
L010 L011 L000 L001 F000 F010 F001 F011 K00 Z10 Z11
L020 F020 F021 K01 Z12 L021 F030 F031 K02 Z13 L030 F040 F041 Z14 L031 K03
L110 L111 S0 F100 F101 F110 F111 L100 L101 K10 Z20 Z21
F120 F121 K11 L120 Z22 L121 F130 F131 K12 Z23 L130 F140 F141 Z24 L131 K13
L210 L211 L220 L221 L230 L231 L200 L201 S1
F200 F201 F210 F211 K20 F220 F221 K21 F230 F231 K22 S2 F240 F241 K23
"""


def divisor(total, most):
    return max(d for d in range(1, most + 1) if total % d == 0)


def groups(low, high, size):
    return [min(at, high - size) for at in range(low, high, size)]


def kernel(
    counts, density, flow_j, flow_i, flow_k, out,
    field, cj, ci, ck, pack, land,
    load_sem, flow_sem, isend, irecv, ksend, krecv, jsend, jrecv,
):
    nj, ni, nk, lanes = density.shape
    deep = nk + 2 * TILE
    n_south, n_east, n_down = counts
    south, east, down = (lax.axis_index(a) for a in ("south", "east", "down"))
    index = {"south": south, "east": east, "down": down}
    has = {
        ("south", 0): (n_south > 1, south > 0),
        ("south", 1): (n_south > 1, south < n_south - 1),
        ("east", 0): (n_east > 1, east > 0),
        ("east", 1): (n_east > 1, east < n_east - 1),
        ("down", 0): (n_down > 1, down > 0),
        ("down", 1): (n_down > 1, down < n_down - 1),
    }
    inside_k = pl.ds(TILE, nk)
    wide = divisor(ni - 2, 6)
    blocks = (ni - 2) // wide
    cut = 1 + wide * (blocks // 2)
    pieces = [(0, cut), (cut, ni)]
    half = max(TILE, nk // 2 // TILE * TILE)
    chunks = [(0, 0, half), (0, half, nk - half)] + [(t, 0, nk) for t in range(1, nj)]

    def neighbour(axis, side):
        return {axis: index[axis] + (1 if side else -1)}

    def when_has(axis, side, act):
        static, dynamic = has[axis, side]
        if static:
            pl.when(dynamic)(act)

    def when_edge(axis, side, act):
        static, dynamic = has[axis, side]
        if static:
            pl.when(jnp.logical_not(dynamic))(act)
        else:
            act()

    first = jnp.where(south == 0, 1, 0) if n_south > 1 else 0

    def plane(t):
        return first * (nj - 1 - t) + (1 - first) * t

    between = pl.ds(1, ni - 2)

    def load(t):
        return pltpu.make_async_copy(
            density.at[plane(t), between],
            field.at[0, plane(t) + 1, pl.ds(2, ni - 2), inside_k],
            load_sem.at[t],
        )

    def load_face(low, rows, high):
        return pltpu.make_async_copy(
            density.at[:, pl.ds(low, rows)],
            field.at[0, pl.ds(1, nj), pl.ds(high, rows), inside_k],
            load_sem.at[nj],
        )

    flows = ((flow_j, cj), (flow_i, ci), (flow_k, ck))

    def load_flow(t, source, target):
        return pltpu.make_async_copy(
            source.at[plane(t), between], target.at[plane(t), between], flow_sem.at[t]
        )

    def load_flow_face(low, rows, source, target):
        return pltpu.make_async_copy(
            source.at[:, pl.ds(low, rows)], target.at[:, pl.ds(low, rows)], flow_sem.at[nj]
        )

    def copy_i(s, side, c):
        t, k, size = chunks[c]
        j, part = plane(t), pl.ds(TILE + k, size)
        return pltpu.make_async_remote_copy(
            src_ref=field.at[s, j + 1, ni if side else 1, part],
            dst_ref=field.at[s, j + 1, 0 if side else ni + 1, part],
            send_sem=isend.at[s % 2, side],
            recv_sem=irecv.at[s % 2, 1 - side, c],
            device_id=neighbour("east", side),
            device_id_type=MESH,
        )

    def copy_k(s, side, j):
        return pltpu.make_async_remote_copy(
            src_ref=pack.at[s, side, j],
            dst_ref=land.at[s, 1 - side, j],
            send_sem=ksend.at[s % 2, side],
            recv_sem=krecv.at[s % 2, 1 - side, j],
            device_id=neighbour("down", side),
            device_id_type=MESH,
        )

    def copy_j(s, side, piece):
        low, high = pieces[piece]
        rows = pl.ds(low + 1, high - low)
        return pltpu.make_async_remote_copy(
            src_ref=field.at[s, nj if side else 1, rows, inside_k],
            dst_ref=field.at[s, 0 if side else nj + 1, rows, inside_k],
            send_sem=jsend.at[s % 2, side],
            recv_sem=jrecv.at[s % 2, 1 - side, piece],
            device_id=neighbour("south", side),
            device_id_type=MESH,
        )

    def send_i(s, c, side, late):
        static, dynamic = has["east", side]
        if static and n_south > 1:
            pl.when(dynamic & ((south > 0) if late else (south == 0)))(copy_i(s, side, c).start)
        elif static and not late:
            pl.when(dynamic)(copy_i(s, side, c).start)

    def send_late(s, c):
        for side in range(2):
            send_i(s, c, side, True)

    def send_k(s, t):
        for side in range(2):
            when_has("down", side, lambda side=side: copy_k(s, side, plane(t)).start())

    def start_j(s, side):
        for piece in range(len(pieces)):
            copy_j(s, side, piece).start()

    def send_j(s, t):
        if n_south > 1 and t == 0:
            pl.when(south == 0)(lambda: start_j(s, 1))
            pl.when(south > 0)(lambda: start_j(s, 0))
        if n_south > 2 and t == nj - 1:
            pl.when((south > 0) & (south < n_south - 1))(lambda: start_j(s, 1))

    waited = set()

    def wait_j(s, t, piece):
        if (s, t, piece) in waited:
            return
        waited.add((s, t, piece))
        if n_south > 1 and t == 0:
            pl.when(south == 0)(lambda: copy_j(s, 0, piece).wait_recv())
            pl.when(south > 0)(lambda: copy_j(s, 1, piece).wait_recv())
        if n_south > 2 and t == nj - 1:
            pl.when((south > 0) & (south < n_south - 1))(
                lambda: copy_j(s, 0, piece).wait_recv()
            )

    def wait_i(s, c, side):
        when_has("east", side, lambda: copy_i(s, 1 - side, c).wait_recv())

    def rows(s, j, i, count, k=0, size=nk):
        def at(dj, di, dk):
            return field[s, j + 1 + dj, i + 1 + di, pl.ds(TILE + k + dk, size), :]

        line = [at(0, r - 1, 0) for r in range(count + 2)]
        for r in range(count):
            cell = (j, i + r, pl.ds(k, size))
            lower = [at(-1, r, 0), line[r], at(0, r, -1)]
            upper = [at(1, r, 0), line[r + 2], at(0, r, 1)]
            gain = [c[cell] for c in (cj, ci, ck)]
            if s == 0:
                gain = [0.05 - g for g in gain]
                for c, g in zip((cj, ci, ck), gain):
                    c[cell] = g
            drift = [g * (u - l) for g, u, l in zip(gain, upper, lower)]
            value = (0.7 * line[r + 1] + 0.1 * (lower[0] + lower[1] + lower[2])) + (
                drift[0] + drift[1] + drift[2]
            )
            if s + 1 < STEPS:
                field[s + 1, j + 1, i + 1 + r, pl.ds(TILE + k, size), :] = value
            else:
                out[cell] = value

    flat = field.reshape(STEPS, nj + 2, (ni + 2) * deep, lanes)
    flat_gain = ck.reshape(nj, ni * nk, lanes)
    flat_out = out.reshape(nj, ni * nk, lanes)

    def edge_field(s, j, i, size, side):
        row = (i + 1) * deep + TILE + (nk - 1) * side
        return flat.at[s, j + 1, pl.ds(row, size, stride=deep), :]

    def edge(ref, j, i, size, side):
        return ref.at[j, pl.ds(i * nk + (nk - 1) * side, size, stride=nk), :]

    def start_flow(t):
        for flow in flows:
            load_flow(t, *flow).start()

    def wait_flow(t):
        pltpu.make_async_copy(
            flow_j.at[pl.ds(0, 3), between], cj.at[pl.ds(0, 3), between], flow_sem.at[t]
        ).wait()
        for later in [2] if t == 1 else range(3, nj) if t == 0 else []:
            start_flow(later)

    def inner(s, t, part):
        if s == 0 and (t, "flow") not in waited:
            waited.add((t, "flow"))
            wait_flow(t)
        edges = (t == 0) or (t == nj - 1 and n_south > 2)
        low, high = [(0, blocks // 2), (blocks // 2, blocks)][part]
        if edges:
            wait_j(s, t, part)

        @pl.loop(low, high)
        def _(b):
            rows(s, plane(t), 1 + b * wide, wide)

    def wait_k(s, t):
        if (s, t, "k") in waited:
            return
        waited.add((s, t, "k"))
        j = plane(t)
        for side in range(2):
            def corner(side=side):
                copy_k(s, 1 - side, j).wait_recv()
                row = TILE + nk if side else TILE - 1
                for i in (0, ni - 1):
                    field[s, j + 1, i + 1, pl.ds(row, 1), :] = land[s, side, j, pl.ds(i, 1), :]
            when_has("down", side, corner)

    def face(s, c, side):
        t, k, size = chunks[c]
        for piece in range(len(pieces)):
            wait_j(s, t, piece)
        wait_k(s, t)
        wait_i(s, c, side)
        rows(s, plane(t), (ni - 1) * side, 1, k, size)
        if s + 1 < STEPS:
            send_i(s + 1, c, side, False)

    def fix(s, t):
        j = plane(t)
        for side in range(2):
            def act(side=side):
                parts = []
                for i in groups(1, ni - 1, TILE):
                    gain = edge(flat_gain, j, i, TILE, side)[...]
                    gain = gain if side else 0.1 - gain
                    if s + 1 < STEPS:
                        target = edge_field(s + 1, j, i, TILE, side)
                    else:
                        target = edge(flat_out, j, i, TILE, side)
                    value = target[...] + gain * land[s, side, j, pl.ds(i, TILE), :]
                    parts.append((i, target, value))
                for i, target, value in parts:
                    target[...] = value
                    if s + 1 < STEPS:
                        pack[s + 1, side, j, pl.ds(i, TILE), :] = value
                if s + 1 < STEPS:
                    k = TILE + (nk - 1) * side
                    for i in (0, ni - 1):
                        pack[s + 1, side, j, pl.ds(i, 1), :] = field[
                            s + 1, j + 1, i + 1, pl.ds(k, 1), :
                        ]
            when_has("down", side, act)
        if s + 1 < STEPS:
            send_k(s + 1, t)
            send_j(s + 1, t)

    def drain(s):
        for side in range(2):
            def sent(side=side):
                pltpu.make_async_remote_copy(
                    src_ref=field.at[s, pl.ds(1, nj), ni if side else 1, inside_k],
                    dst_ref=field.at[s, pl.ds(1, nj), 0 if side else ni + 1, inside_k],
                    send_sem=isend.at[s % 2, side],
                    recv_sem=irecv.at[s % 2, 1 - side, 0],
                    device_id=neighbour("east", side),
                    device_id_type=MESH,
                ).wait_send()
            when_has("east", side, sent)

            def sent(side=side):
                pltpu.make_async_remote_copy(
                    src_ref=pack.at[s, side],
                    dst_ref=land.at[s, 1 - side],
                    send_sem=ksend.at[s % 2, side],
                    recv_sem=krecv.at[s % 2, 1 - side, 0],
                    device_id=neighbour("down", side),
                    device_id_type=MESH,
                ).wait_send()
            when_has("down", side, sent)

            def sent(side=side):
                rows = pl.ds(1, ni)
                pltpu.make_async_remote_copy(
                    src_ref=field.at[s, nj if side else 1, rows, inside_k],
                    dst_ref=field.at[s, 0 if side else nj + 1, rows, inside_k],
                    send_sem=jsend.at[s % 2, side],
                    recv_sem=jrecv.at[s % 2, 1 - side, 0],
                    device_id=neighbour("south", side),
                    device_id_type=MESH,
                ).wait_send()
            when_has("south", side, sent)

    def wait_load(t):
        load(t).wait()

    def pack_first(t):
        for side in range(2):
            def act(side=side):
                for i in groups(0, ni, TILE):
                    pack[0, side, plane(t), pl.ds(i, TILE), :] = edge_field(
                        0, plane(t), i, TILE, side
                    )[...]
            when_has("down", side, act)

    def wait_barrier():
        pl.semaphore_wait(barrier, sum(jnp.where(d, 1, 0) for s, d in has.values() if s))

    def wait_face():
        load_face(0, 2, 1).wait()

    def wait_flow_face():
        load_flow_face(0, 6, flow_j, cj).wait()

    barrier = pltpu.get_barrier_semaphore()
    for axis, side in has:
        def greet(axis=axis, side=side):
            pl.semaphore_signal(
                barrier, inc=1, device_id=neighbour(axis, side), device_id_type=MESH
            )
        when_has(axis, side, greet)

    for low in (0, ni - 1):
        load_face(low, 1, low + 1).start()
    for t in range(nj):
        load(t).start()

    def clear():
        zero_row = jnp.zeros((TILE, lanes), jnp.float32)
        zero_line = jnp.zeros((nk, lanes), jnp.float32)
        for s in range(STEPS):
            @pl.loop(0, nj)
            def _(j):
                for i in groups(0, ni, TILE):
                    for row in (TILE - 1, TILE + nk):
                        flat[s, j + 1, pl.ds((i + 1) * deep + row, TILE, stride=deep), :] = zero_row

        for side in range(2):
            def zero_j(side=side):
                for s in range(STEPS):
                    @pl.loop(0, ni)
                    def _(i):
                        field[s, (nj + 1) * side, i + 1, inside_k, :] = zero_line

            def zero_i(side=side):
                for s in range(STEPS):
                    @pl.loop(0, nj)
                    def _(j):
                        field[s, j + 1, (ni + 1) * side, inside_k, :] = zero_line

            when_edge("south", side, zero_j)
            when_edge("east", side, zero_i)

    clear()
    for flow in flows:
        for low in (0, ni - 1):
            load_flow_face(low, 1, *flow).start()
    start_flow(1)
    wait_barrier()
    wait_face()
    for c in range(len(chunks)):
        for side in range(2):
            send_i(0, c, side, False)
    start_flow(0)
    for t in range(nj):
        if t == 2:
            for c in range(len(chunks)):
                send_late(0, c)
        wait_load(t)
        pack_first(t)
        send_k(0, t)
        send_j(0, t)
    wait_flow_face()

    def order():
        if nj == 4:
            for word in PLAN.split():
                yield word[0], *map(int, word[1:])
            return
        for s in range(STEPS):
            for t in [*range(1, nj), 0]:
                for part in range(2):
                    yield "L", s, t, part
            yield "S", s
            for c, (t, k, size) in enumerate(chunks):
                for side in range(2):
                    yield "F", s, c, side
                if s + 1 < STEPS:
                    yield "Z", s + 1, c
                if k + size == nk:
                    yield "K", s, t

    acts = {"L": inner, "F": face, "K": fix, "S": drain, "Z": send_late}
    for name, *where in order():
        acts[name](*where)


def per_device(counts, density, flow_j, flow_i, flow_k):
    nj, ni, nk, lanes = density.shape
    f32 = jnp.float32
    dma = pltpu.SemaphoreType.DMA
    return pl.pallas_call(
        functools.partial(kernel, counts),
        out_shape=pltpu.VMEM(density.shape, f32),
        in_specs=[pl.BlockSpec(memory_space=pl.ANY)] * 4,
        out_specs=pl.BlockSpec(memory_space=pltpu.VMEM),
        scratch_shapes=[
            pltpu.VMEM((STEPS, nj + 2, ni + 2, nk + 2 * TILE, lanes), f32),
            pltpu.VMEM((nj, ni, nk, lanes), f32),
            pltpu.VMEM((nj, ni, nk, lanes), f32),
            pltpu.VMEM((nj, ni, nk, lanes), f32),
            pltpu.VMEM((STEPS, 2, nj, ni, lanes), f32),
            pltpu.VMEM((STEPS, 2, nj, ni, lanes), f32),
            dma((nj + 1,)),
            dma((nj + 1,)),
            dma((2, 2)),
            dma((2, 2, nj + 1)),
            dma((2, 2)),
            dma((2, 2, nj)),
            dma((2, 2)),
            dma((2, 2, 2)),
        ],
        compiler_params=pltpu.CompilerParams(
            collective_id=0, has_side_effects=True, vmem_limit_bytes=58 * 1024 * 1024
        ),
    )(density, flow_j, flow_i, flow_k)


def solution(mesh):
    spec = P(("ens", "south"), "east", "down", None)
    counts = tuple(mesh.shape[a] for a in ("south", "east", "down"))
    return jax.shard_map(
        functools.partial(per_device, counts),
        mesh=mesh,
        in_specs=(spec,) * 4,
        out_specs=spec,
        check_vma=False,
    )
```

time: 21.5 us -> 18.4 us (0.86)
  Pallas kernels: 19.4 us -> 16.3 us
    pallas_call x1, Pallas kernels: 19.4 us -> 16.3 us  [per_device(): pl.pallas_call(functools.partial(kernel, counts), out_shape=pltpu.VMEM(de...]
where the time goes in v1:
time: 18.4 us; the launch traced here: 18.3 us
  Pallas kernels  16.3 us (89%)
  local copies, waits for them, and re-layouts  2.02 us (11%)
    pallas_call x1, Pallas kernels, per_device(): pl.pallas_call(functools.partial(kernel, counts), out_shape=pltpu.VMEM(de...  16.3 us
    unnamed x1, local copies, waits for them, and re-layouts  2.02 us

profile of v1, /device:TPU:0, one launch (start us, length us, event | category | flops | bytes accessed | tf_op | source)
XLA Modules:
  0.0 18.3 jit_solution(15480846063259915197)
XLA Ops:
  0.0 16.3 %shard_map.46 = f32[4,32,64,128]{3,2,1,0:T(8,128)S(1)} custom-call(f32[4,32,64,128]{3,2,1,0:T(8,128)} %density.1, f32[4,32,64,128]{3,2,1,0:T(8,128)} %flow_j.1, f32[4,32,64,128]{3,2,1,0:T(8,128)} %flow_i.1, f32[4,32,64,128]{3,2,1,0:T(8,128)} %flow_k.1), custom_call_target="tpu_custom_call" | custom-call | tf_op jit(solution)/shard_map/pallas_call | solution.py:436
  16.3 2.0 %copy.6 = f32[4,32,64,128]{3,2,1,0:T(8,128)} copy(f32[4,32,64,128]{3,2,1,0:T(8,128)S(1)} %shard_map.46) | data formatting | bytes 8388608

commit v2 on v1

--- a/solution.py
+++ b/solution.py
@@ -10,14 +10,15 @@
 STEPS = 3
 TILE = 8
 MESH = pl.DeviceIdType.MESH
-PLAN = """
-L010 L011 L000 L001 F000 F010 F001 F011 K00 Z10 Z11
-L020 F020 F021 K01 Z12 L021 F030 F031 K02 Z13 L030 F040 F041 Z14 L031 K03
-L110 L111 S0 F100 F101 F110 F111 L100 L101 K10 Z20 Z21
-F120 F121 K11 L120 Z22 L121 F130 F131 K12 Z23 L130 F140 F141 Z24 L131 K13
-L210 L211 L220 L221 L230 L231 L200 L201 S1
-F200 F201 F210 F211 K20 F220 F221 K21 F230 F231 K22 S2 F240 F241 K23
-"""
+PLAN = (
+    "E01", "M01", "P1", "F000", "F010", "P0", "F001", "F011", "K00", "J1", "Z10", "Z11",
+    "E02", "F020", "F021", "K01", "Z12", "F030", "F040", "F031", "K02", "Z13", "E03", "F041",
+    "K03", "Z14", "M02", "M03", "X1", "E11", "D0", "F100", "F110", "F101", "F111", "E10",
+    "K10", "Z20", "Z21", "M10", "J2", "F120", "F121", "K11", "Z22", "E12", "M11", "F130",
+    "E13", "F140", "F131", "K12", "Z23", "F141", "K13", "Z24", "M12", "M13", "X2", "E21",
+    "M21", "E22", "M22", "E23", "M23", "E20", "M20", "D1", "F200", "F201", "F210", "F211",
+    "K20", "F220", "F221", "K21", "F230", "F231", "K22", "F240", "K23", "D2", "F241",
+)
 
 
 def divisor(total, most):
@@ -47,12 +48,14 @@
         ("down", 1): (n_down > 1, down < n_down - 1),
     }
     inside_k = pl.ds(TILE, nk)
-    wide = divisor(ni - 2, 6)
-    blocks = (ni - 2) // wide
-    cut = 1 + wide * (blocks // 2)
-    pieces = [(0, cut), (cut, ni)]
+    wide = divisor(ni - 2, 10)
+    tall = divisor(ni - 2, 30)
+    pieces = [(0, ni // 2), (ni // 2, ni)]
     half = max(TILE, nk // 2 // TILE * TILE)
     chunks = [(0, 0, half), (0, half, nk - half)] + [(t, 0, nk) for t in range(1, nj)]
+
+    def slot(axis, side):
+        return side if counts[("south", "east", "down").index(axis)] > 2 else 0
 
     def neighbour(axis, side):
         return {axis: index[axis] + (1 if side else -1)}
@@ -92,14 +95,17 @@
 
     flows = ((flow_j, cj), (flow_i, ci), (flow_k, ck))
 
+    def flow_slot(t):
+        return flow_sem.at[t] if t < 2 else load_sem.at[t - 2]
+
     def load_flow(t, source, target):
         return pltpu.make_async_copy(
-            source.at[plane(t), between], target.at[plane(t), between], flow_sem.at[t]
+            source.at[plane(t), between], target.at[plane(t), between], flow_slot(t)
         )
 
     def load_flow_face(low, rows, source, target):
         return pltpu.make_async_copy(
-            source.at[:, pl.ds(low, rows)], target.at[:, pl.ds(low, rows)], flow_sem.at[nj]
+            source.at[:, pl.ds(low, rows)], target.at[:, pl.ds(low, rows)], flow_sem.at[2]
         )
 
     def copy_i(s, side, c):
@@ -118,8 +124,8 @@
         return pltpu.make_async_remote_copy(
             src_ref=pack.at[s, side, j],
             dst_ref=land.at[s, 1 - side, j],
-            send_sem=ksend.at[s % 2, side],
-            recv_sem=krecv.at[s % 2, 1 - side, j],
+            send_sem=ksend.at[s % 2, slot("down", side)],
+            recv_sem=krecv.at[s % 2, slot("down", 1 - side), j],
             device_id=neighbour("down", side),
             device_id_type=MESH,
         )
@@ -130,8 +136,8 @@
         return pltpu.make_async_remote_copy(
             src_ref=field.at[s, nj if side else 1, rows, inside_k],
             dst_ref=field.at[s, 0 if side else nj + 1, rows, inside_k],
-            send_sem=jsend.at[s % 2, side],
-            recv_sem=jrecv.at[s % 2, 1 - side, piece],
+            send_sem=jsend.at[slot("south", side)],
+            recv_sem=jrecv.at[s % 2, slot("south", 1 - side), piece],
             device_id=neighbour("south", side),
             device_id_type=MESH,
         )
@@ -155,11 +161,13 @@
         for piece in range(len(pieces)):
             copy_j(s, side, piece).start()
 
-    def send_j(s, t):
-        if n_south > 1 and t == 0:
+    def send_j(s):
+        if n_south > 1:
             pl.when(south == 0)(lambda: start_j(s, 1))
             pl.when(south > 0)(lambda: start_j(s, 0))
-        if n_south > 2 and t == nj - 1:
+
+    def send_far_j(s):
+        if n_south > 2:
             pl.when((south > 0) & (south < n_south - 1))(lambda: start_j(s, 1))
 
     waited = set()
@@ -219,23 +227,32 @@
 
     def wait_flow(t):
         pltpu.make_async_copy(
-            flow_j.at[pl.ds(0, 3), between], cj.at[pl.ds(0, 3), between], flow_sem.at[t]
+            flow_j.at[pl.ds(0, 3), between], cj.at[pl.ds(0, 3), between], flow_slot(t)
         ).wait()
         for later in [2] if t == 1 else range(3, nj) if t == 0 else []:
             start_flow(later)
 
-    def inner(s, t, part):
+    def ready(s, t):
         if s == 0 and (t, "flow") not in waited:
             waited.add((t, "flow"))
             wait_flow(t)
-        edges = (t == 0) or (t == nj - 1 and n_south > 2)
-        low, high = [(0, blocks // 2), (blocks // 2, blocks)][part]
-        if edges:
-            wait_j(s, t, part)
-
-        @pl.loop(low, high)
+        for piece in range(len(pieces)):
+            wait_j(s, t, piece)
+
+    def edge_tiles(s, t):
+        ready(s, t)
+
+        @pl.loop(0, (ni - 2) // tall)
         def _(b):
-            rows(s, plane(t), 1 + b * wide, wide)
+            for k in sorted({0, nk - TILE}):
+                rows(s, plane(t), 1 + b * tall, tall, k, TILE)
+
+    def middle(s, t):
+        ready(s, t)
+        if nk > 2 * TILE:
+            @pl.loop(0, (ni - 2) // wide)
+            def _(b):
+                rows(s, plane(t), 1 + b * wide, wide, TILE, nk - 2 * TILE)
 
     def wait_k(s, t):
         if (s, t, "k") in waited:
@@ -255,6 +272,9 @@
         for piece in range(len(pieces)):
             wait_j(s, t, piece)
         wait_k(s, t)
+        if s == 0 and "faces" not in waited:
+            waited.add("faces")
+            wait_flow_face()
         wait_i(s, c, side)
         rows(s, plane(t), (ni - 1) * side, 1, k, size)
         if s + 1 < STEPS:
@@ -287,9 +307,8 @@
             when_has("down", side, act)
         if s + 1 < STEPS:
             send_k(s + 1, t)
-            send_j(s + 1, t)
-
-    def drain(s):
+
+    def drain_i(s):
         for side in range(2):
             def sent(side=side):
                 pltpu.make_async_remote_copy(
@@ -302,28 +321,36 @@
                 ).wait_send()
             when_has("east", side, sent)
 
+    def drain_k(s):
+        for side in range(2):
             def sent(side=side):
                 pltpu.make_async_remote_copy(
                     src_ref=pack.at[s, side],
                     dst_ref=land.at[s, 1 - side],
-                    send_sem=ksend.at[s % 2, side],
-                    recv_sem=krecv.at[s % 2, 1 - side, 0],
+                    send_sem=ksend.at[s % 2, slot("down", side)],
+                    recv_sem=krecv.at[s % 2, slot("down", 1 - side), 0],
                     device_id=neighbour("down", side),
                     device_id_type=MESH,
                 ).wait_send()
             when_has("down", side, sent)
 
+    def drain_j(s):
+        for side in range(2):
             def sent(side=side):
                 rows = pl.ds(1, ni)
                 pltpu.make_async_remote_copy(
                     src_ref=field.at[s, nj if side else 1, rows, inside_k],
                     dst_ref=field.at[s, 0 if side else nj + 1, rows, inside_k],
-                    send_sem=jsend.at[s % 2, side],
-                    recv_sem=jrecv.at[s % 2, 1 - side, 0],
+                    send_sem=jsend.at[slot("south", side)],
+                    recv_sem=jrecv.at[s % 2, slot("south", 1 - side), 0],
                     device_id=neighbour("south", side),
                     device_id_type=MESH,
                 ).wait_send()
             when_has("south", side, sent)
+
+    def drain(s):
+        drain_i(s)
+        drain_k(s)
 
     def wait_load(t):
         load(t).wait()
@@ -386,16 +413,12 @@
             when_edge("east", side, zero_i)
 
     clear()
-    for flow in flows:
-        for low in (0, ni - 1):
-            load_flow_face(low, 1, *flow).start()
     start_flow(1)
     wait_barrier()
     wait_face()
     for c in range(len(chunks)):
         for side in range(2):
             send_i(0, c, side, False)
-    start_flow(0)
     for t in range(nj):
         if t == 2:
             for c in range(len(chunks)):
@@ -403,19 +426,27 @@
         wait_load(t)
         pack_first(t)
         send_k(0, t)
-        send_j(0, t)
-    wait_flow_face()
+        if t == 0:
+            send_j(0)
+        if t == nj - 1:
+            send_far_j(0)
+        if t == 0:
+            for flow in flows:
+                for low in (0, ni - 1):
+                    load_flow_face(low, 1, *flow).start()
+            start_flow(0)
 
     def order():
         if nj == 4:
-            for word in PLAN.split():
+            for word in PLAN:
                 yield word[0], *map(int, word[1:])
             return
         for s in range(STEPS):
             for t in [*range(1, nj), 0]:
-                for part in range(2):
-                    yield "L", s, t, part
-            yield "S", s
+                yield "E", s, t
+                yield "M", s, t
+            if s:
+                yield "D", s - 1
             for c, (t, k, size) in enumerate(chunks):
                 for side in range(2):
                     yield "F", s, c, side
@@ -423,16 +454,47 @@
                     yield "Z", s + 1, c
                 if k + size == nk:
                     yield "K", s, t
-
-    acts = {"L": inner, "F": face, "K": fix, "S": drain, "Z": send_late}
+                if k + size == nk and t == 0 and s + 1 < STEPS:
+                    yield "J", s + 1
+            if s + 1 < STEPS:
+                yield "X", s + 1
+        yield "D", STEPS - 1
+
+    def plane_at_end(low_end):
+        def act():
+            edge_tiles(0, 0)
+            middle(0, 0)
+
+        if n_down == 1:
+            if low_end:
+                act()
+            return
+        for piece in range(len(pieces)):
+            wait_j(0, 0, piece)
+        before = set(waited)
+        pl.when((down == 0) if low_end else (down > 0))(act)
+        if low_end:
+            waited.clear()
+            waited.update(before)
+
+    def near(s):
+        drain_j(s - 1)
+        send_j(s)
+
+    acts = {
+        "E": edge_tiles, "M": middle, "F": face, "K": fix,
+        "D": drain, "Z": send_late, "J": near, "X": send_far_j, "P": plane_at_end,
+    }
     for name, *where in order():
         acts[name](*where)
+    drain_j(STEPS - 1)
 
 
 def per_device(counts, density, flow_j, flow_i, flow_k):
     nj, ni, nk, lanes = density.shape
     f32 = jnp.float32
     dma = pltpu.SemaphoreType.DMA
+    south, down = (2 if counts[at] > 2 else 1 for at in (0, 2))
     return pl.pallas_call(
         functools.partial(kernel, counts),
         out_shape=pltpu.VMEM(density.shape, f32),
@@ -446,13 +508,13 @@
             pltpu.VMEM((STEPS, 2, nj, ni, lanes), f32),
             pltpu.VMEM((STEPS, 2, nj, ni, lanes), f32),
             dma((nj + 1,)),
-            dma((nj + 1,)),
+            dma((3,)),
             dma((2, 2)),
             dma((2, 2, nj + 1)),
-            dma((2, 2)),
-            dma((2, 2, nj)),
-            dma((2, 2)),
-            dma((2, 2, 2)),
+            dma((2, down)),
+            dma((2, down, nj)),
+            dma((south,)),
+            dma((2, south, 2)),
         ],
         compiler_params=pltpu.CompilerParams(
             collective_id=0, has_side_effects=True, vmem_limit_bytes=58 * 1024 * 1024

time: 18.4 us -> 18 us (0.978)
  Pallas kernels: 16.3 us -> 15.8 us
    pallas_call x1, Pallas kernels: 16.3 us -> 15.8 us  [per_device(): pl.pallas_call(functools.partial(kernel, counts), out_shape=pltpu.VMEM(de...]
where the time goes in v2:
time: 18 us; the launch traced here: 17.9 us
  Pallas kernels  15.8 us (88%)
  local copies, waits for them, and re-layouts  2.02 us (11%)
    pallas_call x1, Pallas kernels, per_device(): pl.pallas_call(functools.partial(kernel, counts), out_shape=pltpu.VMEM(de...  15.8 us
    unnamed x1, local copies, waits for them, and re-layouts  2.02 us

profile of v2, /device:TPU:0, one launch (start us, length us, event | category | flops | bytes accessed | tf_op | source)
XLA Modules:
  0.0 17.9 jit_solution(9918013687582157688)
XLA Ops:
  0.0 15.8 %shard_map.46 = f32[4,32,64,128]{3,2,1,0:T(8,128)S(1)} custom-call(f32[4,32,64,128]{3,2,1,0:T(8,128)} %density.1, f32[4,32,64,128]{3,2,1,0:T(8,128)} %flow_j.1, f32[4,32,64,128]{3,2,1,0:T(8,128)} %flow_i.1, f32[4,32,64,128]{3,2,1,0:T(8,128)} %flow_k.1), custom_call_target="tpu_custom_call" | custom-call | tf_op jit(solution)/shard_map/pallas_call | solution.py:498
  15.8 2.0 %copy.6 = f32[4,32,64,128]{3,2,1,0:T(8,128)} copy(f32[4,32,64,128]{3,2,1,0:T(8,128)S(1)} %shard_map.46) | data formatting | bytes 8388608

commit v3 on v2

--- a/solution.py
+++ b/solution.py
@@ -13,11 +13,11 @@
 PLAN = (
     "E01", "M01", "P1", "F000", "F010", "P0", "F001", "F011", "K00", "J1", "Z10", "Z11",
     "E02", "F020", "F021", "K01", "Z12", "F030", "F040", "F031", "K02", "Z13", "E03", "F041",
-    "K03", "Z14", "M02", "M03", "X1", "E11", "D0", "F100", "F110", "F101", "F111", "E10",
-    "K10", "Z20", "Z21", "M10", "J2", "F120", "F121", "K11", "Z22", "E12", "M11", "F130",
-    "E13", "F140", "F131", "K12", "Z23", "F141", "K13", "Z24", "M12", "M13", "X2", "E21",
-    "M21", "E22", "M22", "E23", "M23", "E20", "M20", "D1", "F200", "F201", "F210", "F211",
-    "K20", "F220", "F221", "K21", "F230", "F231", "K22", "F240", "K23", "D2", "F241",
+    "K03", "Z14", "M02", "M03", "X1", "A11", "B11", "D0", "F100", "F101", "F110", "F111",
+    "Z20", "Z21", "E10", "K10", "M10", "J2", "C11", "F120", "F121", "K11", "Z22", "E12",
+    "F130", "E13", "F140", "F131", "K12", "Z23", "F141", "K13", "Z24", "M12", "M13", "X2",
+    "E21", "M21", "E22", "M22", "E23", "M23", "E20", "M20", "D1", "F200", "F201", "F210",
+    "F211", "K20", "F220", "F221", "K21", "F230", "F231", "K22", "F240", "K23", "D2", "F241",
 )
 
 
@@ -51,7 +51,7 @@
     wide = divisor(ni - 2, 10)
     tall = divisor(ni - 2, 30)
     pieces = [(0, ni // 2), (ni // 2, ni)]
-    half = max(TILE, nk // 2 // TILE * TILE)
+    half = max(TILE, nk * 3 // 4 // TILE * TILE)
     chunks = [(0, 0, half), (0, half, nk - half)] + [(t, 0, nk) for t in range(1, nj)]
 
     def slot(axis, side):
@@ -254,24 +254,28 @@
             def _(b):
                 rows(s, plane(t), 1 + b * wide, wide, TILE, nk - 2 * TILE)
 
-    def wait_k(s, t):
-        if (s, t, "k") in waited:
+    def wait_k(s, t, side):
+        if (s, t, side, "k") in waited:
             return
-        waited.add((s, t, "k"))
+        waited.add((s, t, side, "k"))
         j = plane(t)
-        for side in range(2):
-            def corner(side=side):
-                copy_k(s, 1 - side, j).wait_recv()
-                row = TILE + nk if side else TILE - 1
-                for i in (0, ni - 1):
-                    field[s, j + 1, i + 1, pl.ds(row, 1), :] = land[s, side, j, pl.ds(i, 1), :]
-            when_has("down", side, corner)
+
+        def corner():
+            copy_k(s, 1 - side, j).wait_recv()
+            row = TILE + nk if side else TILE - 1
+            for i in (0, ni - 1):
+                field[s, j + 1, i + 1, pl.ds(row, 1), :] = land[s, side, j, pl.ds(i, 1), :]
+
+        when_has("down", side, corner)
 
     def face(s, c, side):
         t, k, size = chunks[c]
         for piece in range(len(pieces)):
             wait_j(s, t, piece)
-        wait_k(s, t)
+        if k == 0:
+            wait_k(s, t, 0)
+        if k + size == nk:
+            wait_k(s, t, 1)
         if s == 0 and "faces" not in waited:
             waited.add("faces")
             wait_flow_face()
@@ -460,34 +464,52 @@
                 yield "X", s + 1
         yield "D", STEPS - 1
 
-    def plane_at_end(low_end):
-        def act():
-            edge_tiles(0, 0)
-            middle(0, 0)
-
-        if n_down == 1:
-            if low_end:
-                act()
-            return
+    def when_end(low_end, act):
+        if n_down > 1:
+            pl.when((down == 0) if low_end else (down > 0))(act)
+        elif low_end:
+            act()
+
+    def whole(s, t):
+        edge_tiles(s, t)
+        middle(s, t)
+
+    def first_plane(low_end):
         for piece in range(len(pieces)):
             wait_j(0, 0, piece)
         before = set(waited)
-        pl.when((down == 0) if low_end else (down > 0))(act)
+        when_end(low_end, lambda: whole(0, 0))
         if low_end:
             waited.clear()
             waited.update(before)
 
+    def low_plane(s, t):
+        when_end(True, lambda: whole(s, t))
+
+    def high_edge(s, t):
+        when_end(False, lambda: edge_tiles(s, t))
+
+    def high_middle(s, t):
+        when_end(False, lambda: middle(s, t))
+
     def near(s):
         drain_j(s - 1)
         send_j(s)
 
     acts = {
         "E": edge_tiles, "M": middle, "F": face, "K": fix,
-        "D": drain, "Z": send_late, "J": near, "X": send_far_j, "P": plane_at_end,
+        "D": drain, "Z": send_late, "J": near, "X": send_far_j,
+        "P": first_plane, "A": low_plane, "B": high_edge, "C": high_middle,
     }
     for name, *where in order():
         acts[name](*where)
     drain_j(STEPS - 1)
+
+
+def store(end, out, sem):
+    for j in range(out.shape[0]):
+        pltpu.make_async_copy(end.at[j], out.at[j], sem).start()
+    pltpu.make_async_copy(end, out, sem).wait()
 
 
 def per_device(counts, density, flow_j, flow_i, flow_k):
@@ -495,7 +517,7 @@
     f32 = jnp.float32
     dma = pltpu.SemaphoreType.DMA
     south, down = (2 if counts[at] > 2 else 1 for at in (0, 2))
-    return pl.pallas_call(
+    end = pl.pallas_call(
         functools.partial(kernel, counts),
         out_shape=pltpu.VMEM(density.shape, f32),
         in_specs=[pl.BlockSpec(memory_space=pl.ANY)] * 4,
@@ -520,6 +542,14 @@
             collective_id=0, has_side_effects=True, vmem_limit_bytes=58 * 1024 * 1024
         ),
     )(density, flow_j, flow_i, flow_k)
+    return pl.pallas_call(
+        store,
+        out_shape=jax.ShapeDtypeStruct(density.shape, f32),
+        in_specs=[pl.BlockSpec(memory_space=pltpu.VMEM)],
+        out_specs=pl.BlockSpec(memory_space=pl.ANY),
+        scratch_shapes=[dma],
+        compiler_params=pltpu.CompilerParams(vmem_limit_bytes=1024 * 1024),
+    )(end)
 
 
 def solution(mesh):

time: 18 us -> 17.8 us (0.989)
  local copies, waits for them, and re-layouts: 2.02 us -> 0 us
  Pallas kernels: 15.8 us -> 17.7 us
    pallas_call x0 -> x1, Pallas kernels: none -> 2.02 us  [per_device(): pl.pallas_call(store, out_shape=jax.ShapeDtypeStruct(density.shape, f32),...]
    unnamed x1 -> x0, local copies, waits for them, and re-layouts: 2.02 us -> none
where the time goes in v3:
time: 17.8 us; the launch traced here: 17.7 us
  Pallas kernels  17.7 us (99%)
    pallas_call x1, Pallas kernels, per_device(): pl.pallas_call(functools.partial(kernel, counts), out_shape=pltpu.VMEM(de...  15.7 us
    pallas_call x1, Pallas kernels, per_device(): pl.pallas_call(store, out_shape=jax.ShapeDtypeStruct(density.shape, f32),...  2.02 us

profile of v3, /device:TPU:0, one launch (start us, length us, event | category | flops | bytes accessed | tf_op | source)
XLA Modules:
  0.0 17.7 jit_solution(3912609917838369254)
XLA Ops:
  0.0 15.7 %shard_map.46.end = f32[4,32,64,128]{3,2,1,0:T(8,128)S(1)} custom-call(f32[4,32,64,128]{3,2,1,0:T(8,128)} %density.1, f32[4,32,64,128]{3,2,1,0:T(8,128)} %flow_j.1, f32[4,32,64,128]{3,2,1,0:T(8,128)} %flow_i.1, f32[4,32,64,128]{3,2,1,0:T(8,128)} %flow_k.1), custom_call_target="tpu_custom_call" | custom-call | tf_op jit(solution)/shard_map/pallas_call | solution.py:520
  15.7 2.0 %shard_map.47 = f32[4,32,64,128]{3,2,1,0:T(8,128)} custom-call(f32[4,32,64,128]{3,2,1,0:T(8,128)S(1)} %shard_map.46.end), custom_call_target="tpu_custom_call" | custom-call | tf_op jit(solution)/shard_map/pallas_call | solution.py:545
